TPU v7x, 32 devices: a whole 2x2x4 slice. The times are simulated.
32 devices in a mesh: dp: 16 (over z, x, core), tp: 2 (over y).
Axes of the slice: x: 2, y: 2, z: 4, core: 2. Of those that a mesh axis runs over, the one named last changes fastest.
Arguments:
- stash_values: bfloat16 [4096, 8192], P(('dp', 'tp')), may hold values from -127 to 127
- stash_scales: bfloat16 [4096, 64], P(('dp', 'tp')), may hold values from 0.001 to 0.13
- value_grad: bfloat16 [4096, 256], P('dp', 'tp'), may hold values from -19 to 19
Outputs:
- clipped_grad: float32 [8192, 256], P('dp', 'tp')
All inputs are finite; a program needn't handle non-finite values.
Results may differ from a plain program's by a relative error of at most 0.0019.
Values may be sent and summed in bfloat16 or wider, within the bound.
No kernel may reach another device: no remote copies, remote signals or barrier semaphores. Data moves between devices by JAX's collectives and lax.ppermute only.
A program may use at most 64 MiB of HBM per device.

v0:
```python
import jax
import jax.numpy as jnp
from jax import lax
from jax.sharding import PartitionSpec as P


def block_dequantize(values, scales):
    rows = values.shape[0]
    blocks = scales.shape[1]
    scaled = (
        values.astype(jnp.float32).reshape(rows, blocks, values.shape[1] // blocks)
        * scales.astype(jnp.float32)[:, :, None]
    )
    return scaled.reshape(rows, values.shape[1]).astype(jnp.bfloat16)


def body(stash_values, stash_scales, value_grad):
    width = stash_values.shape[1]
    columns = value_grad.shape[1]
    dp_count = lax.axis_size("dp")
    tp_count = lax.axis_size("tp")
    own_tokens = stash_values.shape[0]
    sub_rows = width // (dp_count * tp_count)
    inputs = block_dequantize(stash_values, stash_scales)
    inputs = inputs.reshape(own_tokens, dp_count, tp_count, sub_rows)
    features = lax.all_to_all(inputs, "tp", split_axis=2, concat_axis=0, tiled=True)
    features = features.reshape(own_tokens * tp_count, dp_count * sub_rows)
    all_heads = lax.dot_general(
        features,
        lax.all_gather(value_grad, "tp", axis=1, tiled=True),
        (((0,), (0,)), ((), ())),
        preferred_element_type=jnp.float32,
    )
    summed = lax.psum_scatter(all_heads, "dp", scatter_dimension=0, tiled=True)
    local = lax.all_to_all(summed, "tp", split_axis=1, concat_axis=0, tiled=True)
    total = lax.psum(jnp.sum(summed * summed), ("dp", "tp"))
    limit = jnp.sqrt(jnp.float32(width * columns * lax.axis_size("tp")))
    return local * jnp.minimum(jnp.float32(1.0), limit / jnp.sqrt(total))


def solution(mesh):
    placed = (P(("dp", "tp"), None), P(("dp", "tp"), None), P("dp", "tp"))
    return jax.shard_map(body, mesh=mesh, in_specs=placed, out_specs=P("dp", "tp"), check_vma=False)
```

profile of v0, /device:TPU:0, one launch (start us, length us, event | category | flops | bytes accessed | tf_op | source)
XLA Modules:
  0.0 181.6 jit_solution(3500669515704277287)
XLA Ops:
  6.5 0.8 copy.9
  7.3 0.0 copy-start
  7.4 1.1 mul.26
  8.5 0.4 copy-done
  8.9 3.8 %fusion = bf16[128,8192]{1,0:T(8,128)(2,1)} fusion(f32[16,8,64,128]{3,2,1,0:T(8,128)S(1)} %bitcast.22, bf16[128,8192]{1,0:T(8,128)(2,1)S(1)} %copy-done), kind=kLoop, calls=%fused_computation.1 | loop fusion | flops 3145728 | bytes 8388608 | tf_op jit(solution)/shard_map/convert_element_type | solution.py:14
  12.7 3.3 %reshape.16 = bf16[128,16,2,256]{3,2,1,0:T(2,128)(2,1)S(1)} reshape(bf16[128,8192]{1,0:T(8,128)(2,1)} %fusion) | data formatting | bytes 4194304 | tf_op jit(solution)/shard_map/reshape | solution.py:25
  16.0 1.7 copy.10
  17.7 0.0 copy-start.1
  17.7 4.4 %all-to-all-start = ((bf16[128,16,2,256]{3,1,0,2:T(8,128)(2,1)}), bf16[128,16,2,256]{3,1,0,2:T(8,128)(2,1)S(1)}, u32[]{:S(2)}, u32[]{:S(2)}) async-start(bf16[128,16,2,256]{3,1,0,2:T(8,128)(2,1)} %copy.10), calls=%async_computation | async-start | bytes 4194304 | tf_op jit(solution)/shard_map/all_to_all | solution.py:26
  22.1 0.0 reduce-scatter.2.cloned.1.call-start
  22.1 0.0 copy-done.1
  22.1 27.3 %all_gather.3 = bf16[256,256]{1,0:T(8,128)(2,1)S(1)} all-gather(bf16[256,128]{1,0:T(8,128)(2,1)S(1)} %copy-done.1), channel_id=1, replica_groups=mesh['dp'=16,'tp'=2] {'tp'}, dimensions={1}, use_global_device_ids=true | all-gather | bytes 196608 | tf_op jit(solution)/shard_map/all_gather | solution.py:30
  49.4 0.0 all-to-all-done
  49.4 0.9 copy.14
  50.3 2.7 %fusion.1 = f32[4096,256]{1,0:T(8,128)} fusion(bf16[256,4096]{1,0:T(8,128)(2,1)S(1)} %bitcast.23, bf16[256,256]{1,0:T(8,128)(2,1)S(1)} %all_gather.3), kind=kOutput, calls=%fused_computation.5 | convolution fusion | flops 536870912 | bytes 6422528 | tf_op jit(solution)/shard_map/dot_general | solution.py:28
  53.0 0.0 reduce-scatter.2.cloned.1.call-update
  53.1 73.4 %reduce-scatter.2.cloned.1.call-done = f32[256,256]{1,0:T(8,128)} async-done(((f32[4096,256]{1,0:T(8,128)}), f32[256,256]{1,0:T(8,128)}) %reduce-scatter.2.cloned.1.call-update) | async-done | bytes 262160 | tf_op jit(solution)/shard_map/reduce_scatter | solution.py:34
  126.5 1.7 copy_bitcast_fusion
  128.2 3.4 %all-to-all-start.1 = ((f32[256,2,128]{2,0,1:T(8,128)}), f32[256,2,128]{2,0,1:T(8,128)S(1)}, u32[]{:S(2)}, u32[]{:S(2)}) async-start(f32[256,2,128]{2,0,1:T(8,128)} %copy_bitcast_fusion), calls=%async_computation.2 | async-start | bytes 524288 | tf_op jit(solution)/shard_map/all_to_all | solution.py:35
  131.6 1.6 multiply_reduce_fusion
  133.2 40.2 %psum.7 = f32[]{:T(128)} all-reduce(f32[]{:T(128)} %multiply_reduce_fusion), channel_id=1, replica_groups=mesh['dp'=16,'tp'=2] {'dp','tp'}, use_global_device_ids=true, to_apply=%region_2.0 | all-reduce | flops 1 | bytes 8 | tf_op jit(solution)/shard_map/psum | solution.py:36
  174.0 0.0 all-to-all-done.1
  174.1 0.7 broadcast_multiply_fusion
Async XLA Ops:
  7.3 1.6 copy-start
  17.7 4.4 %copy-start.1 = (bf16[256,128]{1,0:T(8,128)(2,1)S(1)}, bf16[256,128]{1,0:T(8,128)(2,1)}, u32[]{:S(2)}) copy-start(bf16[256,128]{1,0:T(8,128)(2,1)} %param.5) | copy-start | bytes 196612
  17.7 31.7 %all-to-all-start = ((bf16[128,16,2,256]{3,1,0,2:T(8,128)(2,1)}), bf16[128,16,2,256]{3,1,0,2:T(8,128)(2,1)S(1)}, u32[]{:S(2)}, u32[]{:S(2)}) async-start(bf16[128,16,2,256]{3,1,0,2:T(8,128)(2,1)} %copy.10), calls=%async_computation | async-start | bytes 4194304 | tf_op jit(solution)/shard_map/all_to_all | solution.py:26
  22.1 104.4 %reduce-scatter.2.cloned.1.call-start = ((), (), s32[]{:S(2)}) async-start(), calls=%async_computation.3 | async-start | bytes 4456448 | tf_op jit(solution)/shard_map/reduce_scatter | solution.py:34
  128.2 45.9 %all-to-all-start.1 = ((f32[256,2,128]{2,0,1:T(8,128)}), f32[256,2,128]{2,0,1:T(8,128)S(1)}, u32[]{:S(2)}, u32[]{:S(2)}) async-start(f32[256,2,128]{2,0,1:T(8,128)} %copy_bitcast_fusion), calls=%async_computation.2 | async-start | bytes 524288 | tf_op jit(solution)/shard_map/all_to_all | solution.py:35
Sparse Core Ops, SparseCore 0:
  53.2 73.2 reduce-scatter.1
where the time goes:
time: 182 us
  waiting for transfers between devices  73.4 us (40%)
  blocking collectives  67.5 us (37%)
  between operations  14 us (8%)
  local copies, waits for them, and re-layouts  9.97 us (5%)
  starting transfers between devices  7.84 us (4%)
  other arithmetic  6.12 us (3%)
  matrix products  2.71 us (1%)
    reduce_scatter x1, waiting for transfers between devices, body(): summed = lax.psum_scatter(all_heads, 'dp', scatter_dimension=0, tiled=True)  73.4 us
    psum x1, blocking collectives, body(): total = lax.psum(jnp.sum(summed * summed), ('dp', 'tp'))  40.2 us
    all_gather x1, blocking collectives, body(): lax.all_gather(value_grad, 'tp', axis=1, tiled=True)  27.3 us
    reshape x2, local copies, waits for them, and re-layouts, body(): inputs = inputs.reshape(own_tokens, dp_count, tp_count, sub_rows)  4.97 us
    all_to_all x1, starting transfers between devices, body(): lax.all_to_all(inputs, 'tp', split_axis=2, concat_axis=0, tiled=True)  4.39 us
    convert_element_type x1, other arithmetic, block_dequantize(): return scaled.reshape(rows, values.shape[1]).astype(jnp.bfloat16)  3.79 us
  transfers between devices with their start and end apart: 3, of which 1 were waited for; matrix products, arithmetic and copies ran while one was open for 1% of the time, Pallas kernels for 0%

commit v1 on v0

--- a/solution.py
+++ b/solution.py
@@ -2,6 +2,13 @@
 import jax.numpy as jnp
 from jax import lax
 from jax.sharding import PartitionSpec as P
+
+
+def keys_supply_all(point, axis_name, array_axis):
+    return jnp.concatenate(
+        lax.all_to_all(jnp.stack([point] * lax.psum(1, axis_name)), axis_name, 0, 0),
+        axis=array_axis,
+    )
 
 
 def block_dequantize(values, scales):
@@ -27,7 +34,7 @@
     features = features.reshape(own_tokens * tp_count, dp_count * sub_rows)
     all_heads = lax.dot_general(
         features,
-        lax.all_gather(value_grad, "tp", axis=1, tiled=True),
+        keys_supply_all(value_grad, "tp", 1),
         (((0,), (0,)), ((), ())),
         preferred_element_type=jnp.float32,
     )

time: 182 us -> 188 us (1.033)
  blocking collectives: 67.5 us -> 40.2 us
  waiting for transfers between devices: 73.4 us -> 100 us
  starting transfers between devices: 7.84 us -> 11.3 us
    all_gather x1 -> x0, blocking collectives: 27.3 us -> none  [body(): lax.all_gather(value_grad, 'tp', axis=1, tiled=True)]
    all_to_all x1, waiting for transfers between devices: 0.01 us -> 25.1 us  [body(): lax.all_to_all(inputs, 'tp', split_axis=2, concat_axis=0, tiled=True)]
    all_to_all x0 -> x1, starting transfers between devices: none -> 3.38 us  [keys_supply_all(): lax.all_to_all(jnp.stack([point] * lax.psum(1, axis_name)), axis_name, 0, 0)]
  transfers between devices with their start and end apart: 3 -> 4, of which waited for: 1 -> 3; matrix products, arithmetic and copies ran while one was open for 1% -> 3% of each run, Pallas kernels for 0% -> 0%
where the time goes in v1:
time: 188 us; the launch traced here: 187 us
  waiting for transfers between devices  100 us (53%)
  blocking collectives  40.2 us (21%)
  between operations  14.1 us (8%)
  local copies, waits for them, and re-layouts  11.7 us (6%)
  starting transfers between devices  11.3 us (6%)
  other arithmetic  6.81 us (4%)
  matrix products  2.71 us (1%)
    reduce_scatter x1, waiting for transfers between devices, body(): summed = lax.psum_scatter(all_heads, 'dp', scatter_dimension=0, tiled=True)  73.4 us
    psum x1, blocking collectives, body(): total = lax.psum(jnp.sum(summed * summed), ('dp', 'tp'))  40.2 us
    all_to_all x1, waiting for transfers between devices, body(): lax.all_to_all(inputs, 'tp', split_axis=2, concat_axis=0, tiled=True)  25.1 us
    reshape x2, local copies, waits for them, and re-layouts, body(): inputs = inputs.reshape(own_tokens, dp_count, tp_count, sub_rows)  4.96 us
    all_to_all x1, starting transfers between devices, body(): lax.all_to_all(inputs, 'tp', split_axis=2, concat_axis=0, tiled=True)  4.39 us
    convert_element_type x1, other arithmetic, block_dequantize(): return scaled.reshape(rows, values.shape[1]).astype(jnp.bfloat16)  3.77 us
  transfers between devices with their start and end apart: 4, of which 3 were waited for; matrix products, arithmetic and copies ran while one was open for 3% of the time, Pallas kernels for 0%

profile of v1, /device:TPU:0, one launch (start us, length us, event | category | flops | bytes accessed | tf_op | source)
XLA Modules:
  0.0 187.2 jit_solution(955448882181115075)
XLA Ops:
  6.5 0.8 copy.10
  7.3 0.0 copy-start.1
  7.4 1.1 mul.26
  8.5 0.4 copy-done.1
  8.9 3.8 %fusion = bf16[128,8192]{1,0:T(8,128)(2,1)} fusion(f32[16,8,64,128]{3,2,1,0:T(8,128)S(1)} %bitcast.26, bf16[128,8192]{1,0:T(8,128)(2,1)S(1)} %copy-done.1), kind=kLoop, calls=%fused_computation.1 | loop fusion | flops 3145728 | bytes 8388608 | tf_op jit(solution)/shard_map/convert_element_type | solution.py:21
  12.7 3.3 %reshape.22 = bf16[128,16,2,256]{3,2,1,0:T(2,128)(2,1)S(1)} reshape(bf16[128,8192]{1,0:T(8,128)(2,1)} %fusion) | data formatting | bytes 4194304 | tf_op jit(solution)/shard_map/reshape | solution.py:32
  16.0 1.7 copy.11
  17.7 0.0 copy-start.2
  17.7 4.4 %all-to-all-start = ((bf16[128,16,2,256]{3,1,0,2:T(8,128)(2,1)}), bf16[128,16,2,256]{3,1,0,2:T(8,128)(2,1)S(1)}, u32[]{:S(2)}, u32[]{:S(2)}) async-start(bf16[128,16,2,256]{3,1,0,2:T(8,128)(2,1)} %copy.11), calls=%async_computation | async-start | bytes 4194304 | tf_op jit(solution)/shard_map/all_to_all | solution.py:33
  22.1 0.0 copy-done.2
  22.1 0.1 copy.12
  22.2 0.7 pad_maximum_fusion
  22.9 25.1 %all-to-all-done = bf16[128,16,2,256]{3,1,0,2:T(8,128)(2,1)S(1)} async-done(((bf16[128,16,2,256]{3,1,0,2:T(8,128)(2,1)}), bf16[128,16,2,256]{3,1,0,2:T(8,128)(2,1)S(1)}, u32[]{:S(2)}, u32[]{:S(2)}) %all-to-all-start) | async-done | bytes 2097184 | tf_op jit(solution)/shard_map/all_to_all | solution.py:33
  47.9 0.0 copy-start
  47.9 3.4 %all-to-all-start.1 = ((bf16[2,256,128]{1,2,0:T(8,128)(2,1)}), bf16[2,256,128]{1,2,0:T(8,128)(2,1)S(1)}, u32[]{:S(2)}, u32[]{:S(2)}) async-start(bf16[2,256,128]{1,2,0:T(8,128)(2,1)} %pad_maximum_fusion), calls=%async_computation.1 | async-start | bytes 262144 | tf_op jit(solution)/shard_map/all_to_all | solution.py:9
  51.3 0.0 reduce-scatter.2.cloned.1.call-start
  51.4 0.0 copy-done
  51.4 2.5 %copy.16 = bf16[32,8,16,256]{3,1,2,0:T(8,128)(2,1)S(1)} copy(bf16[32,8,16,256]{3,2,1,0:T(8,128)(2,1)} %bitcast.28) | data formatting | bytes 4194304
  53.9 1.9 all-to-all-done.1
  55.8 2.7 %fusion.1 = f32[4096,256]{1,0:T(8,128)} fusion(bf16[256,4096]{1,0:T(8,128)(2,1)S(1)} %bitcast.27, bf16[256,256]{0,1:T(8,128)(2,1)S(1)} %bitcast.29), kind=kOutput, calls=%fused_computation.6 | convolution fusion | flops 536870912 | bytes 6422528 | tf_op jit(solution)/shard_map/dot_general | solution.py:35
  58.5 0.0 reduce-scatter.2.cloned.1.call-update
  58.5 73.4 %reduce-scatter.2.cloned.1.call-done = f32[256,256]{1,0:T(8,128)} async-done(((f32[4096,256]{1,0:T(8,128)}), f32[256,256]{1,0:T(8,128)}) %reduce-scatter.2.cloned.1.call-update) | async-done | bytes 262160 | tf_op jit(solution)/shard_map/reduce_scatter | solution.py:41
  131.9 1.7 copy_bitcast_fusion
  133.6 3.4 %all-to-all-start.2 = ((f32[256,2,128]{2,0,1:T(8,128)}), f32[256,2,128]{2,0,1:T(8,128)S(1)}, u32[]{:S(2)}, u32[]{:S(2)}) async-start(f32[256,2,128]{2,0,1:T(8,128)} %copy_bitcast_fusion), calls=%async_computation.3 | async-start | bytes 524288 | tf_op jit(solution)/shard_map/all_to_all | solution.py:42
  137.1 1.7 multiply_reduce_fusion
  138.7 40.2 %psum.7 = f32[]{:T(128)} all-reduce(f32[]{:T(128)} %multiply_reduce_fusion), channel_id=1, replica_groups=mesh['dp'=16,'tp'=2] {'dp','tp'}, use_global_device_ids=true, to_apply=%region_2.0 | all-reduce | flops 1 | bytes 8 | tf_op jit(solution)/shard_map/psum | solution.py:43
  179.6 0.0 all-to-all-done.2
  179.6 0.7 broadcast_multiply_fusion
Async XLA Ops:
  7.3 1.6 copy-start.1
  17.7 4.4 %copy-start.2 = (bf16[256,128]{1,0:T(8,128)(2,1)S(1)}, bf16[256,128]{1,0:T(8,128)(2,1)}, u32[]{:S(2)}) copy-start(bf16[256,128]{1,0:T(8,128)(2,1)} %param.5) | copy-start | bytes 196612
  17.7 30.2 %all-to-all-start = ((bf16[128,16,2,256]{3,1,0,2:T(8,128)(2,1)}), bf16[128,16,2,256]{3,1,0,2:T(8,128)(2,1)S(1)}, u32[]{:S(2)}, u32[]{:S(2)}) async-start(bf16[128,16,2,256]{3,1,0,2:T(8,128)(2,1)} %copy.11), calls=%async_computation | async-start | bytes 4194304 | tf_op jit(solution)/shard_map/all_to_all | solution.py:33
  47.9 3.4 %copy-start = (bf16[128,16,2,256]{3,1,0,2:T(8,128)(2,1)}, bf16[128,16,2,256]{3,1,0,2:T(8,128)(2,1)S(1)}, u32[]{:S(2)}) copy-start(bf16[128,16,2,256]{3,1,0,2:T(8,128)(2,1)S(1)} %all-to-all-done) | copy-start | bytes 6291460
  47.9 7.8 %all-to-all-start.1 = ((bf16[2,256,128]{1,2,0:T(8,128)(2,1)}), bf16[2,256,128]{1,2,0:T(8,128)(2,1)S(1)}, u32[]{:S(2)}, u32[]{:S(2)}) async-start(bf16[2,256,128]{1,2,0:T(8,128)(2,1)} %pad_maximum_fusion), calls=%async_computation.1 | async-start | bytes 262144 | tf_op jit(solution)/shard_map/all_to_all | solution.py:9
  51.3 80.6 %reduce-scatter.2.cloned.1.call-start = ((), (), s32[]{:S(2)}) async-start(), calls=%async_computation.4 | async-start | bytes 4456448 | tf_op jit(solution)/shard_map/reduce_scatter | solution.py:41
  133.6 46.0 %all-to-all-start.2 = ((f32[256,2,128]{2,0,1:T(8,128)}), f32[256,2,128]{2,0,1:T(8,128)S(1)}, u32[]{:S(2)}, u32[]{:S(2)}) async-start(f32[256,2,128]{2,0,1:T(8,128)} %copy_bitcast_fusion), calls=%async_computation.3 | async-start | bytes 524288 | tf_op jit(solution)/shard_map/all_to_all | solution.py:42
Sparse Core Ops, SparseCore 0:
  58.6 73.2 reduce-scatter.1
